TPU v7x, 128 devices: a whole 4x4x4 slice. The times are simulated.
128 devices in a mesh: rec: 4 (over z), space: 32 (over y, x, core).
Axes of the slice: x: 4, y: 4, z: 4, core: 2. Of those that a mesh axis runs over, the one named last changes fastest.
Arguments:
- probes: bfloat16 [1048576, 128], P('space'), may hold values from -6 to 6
- band_coeffs: bfloat16 [16, 8, 1048576], P('rec', None, 'space'), may hold values from -2 to 2
- band_offsets: int32 [16, 8], P('rec'), may hold values from -128 to 128, as said below
Outputs:
- q_basis: float32 [1048576, 128], P(('space', 'rec'))
- r_factor: float32 [128, 128], replicated
Inputs may be any that keep to these rules, and one draw needn't show every extreme that they name: `band_offsets`: in every record band 0 has offset -128 and band 1 offset 128.
All inputs are finite; a program needn't handle non-finite values.
Results may differ from a plain program's by a relative error of at most 0.0003.
Values may be sent and summed in bfloat16 or wider, within the bound.
A program may use at most 128 MiB of HBM per device.

v0:
```python
import jax
import jax.numpy as jnp
from jax import lax
from jax.sharding import PartitionSpec as P

HALO = 128


def padded_2(cells, sides, width):
    for axis, dim in sides:
        count = lax.axis_size(axis)
        ends = count - 1
        head = lax.slice_in_dim(cells, 0, width, axis=dim)
        tail = lax.slice_in_dim(cells, cells.shape[dim] - width, cells.shape[dim], axis=dim)
        cells = jnp.concatenate(
            [
                lax.ppermute(tail, axis, [(i, (i + 1) % count) for i in range(ends)]),
                cells,
                lax.ppermute(head, axis, [((i + 1) % count, i) for i in range(ends)]),
            ],
            axis=dim,
        )
    return cells


def accumulate(padded, coeffs, offsets, row_start, count, margin):
    width = padded.shape[1]
    total = jnp.zeros((count, width), jnp.float32)
    for record in range(coeffs.shape[0]):
        for band in range(coeffs.shape[1]):
            offset = offsets[record, band]
            piece = lax.dynamic_slice_in_dim(padded, row_start + margin + offset, count, 0)
            coeff = coeffs[record, band]
            total = total + coeff.astype(jnp.float32)[:, None] * piece.astype(jnp.float32)
    return total


def local(probes, band_coeffs, band_offsets):
    rows = probes.shape[0]
    margin = HALO
    padded = padded_2(probes, (("space", 0),), margin)
    share = rows // lax.axis_size("rec")
    sketch = lax.psum_scatter(
        accumulate(
            padded, band_coeffs, band_offsets, jnp.int32(0), lax.axis_size("rec") * share, margin
        ),
        "rec",
        scatter_dimension=0,
        tiled=True,
    )
    local_gram = jnp.dot(
        sketch.T, sketch, precision=lax.Precision.HIGHEST, preferred_element_type=jnp.float32
    )
    gram = lax.psum(local_gram, ("rec", "space"))
    upper = jnp.linalg.cholesky(gram).T
    scale = jnp.sqrt(jnp.float32(rows * lax.axis_size("space")))
    solved = jax.scipy.linalg.solve_triangular(upper.T, sketch.T, lower=True)
    return (solved.T * scale, upper / scale)


def solution(mesh):
    in_specs = (P("space", None), P("rec", None, "space"), P("rec", None))
    out_specs = (P(("space", "rec"), None), P())
    return jax.shard_map(local, mesh=mesh, in_specs=in_specs, out_specs=out_specs, check_vma=False)
```

profile of v0, /device:TPU:1, one launch (start us, length us, event | category | flops | bytes accessed | tf_op | source)
XLA Modules:
  0.0 890.0 jit_solution(6260652256925387998)
XLA Ops:
  7.2 0.0 reduce-scatter.2.cloned.1.call-start
  7.2 1.4 fusion.2
  8.6 3.3 collective-permute-start.1
  11.9 3.1 collective-permute-start
  15.0 5.8 slice_convert_fusion.30
  20.8 6.8 slice_convert_fusion.31
  27.6 2.1 fusion.3
  29.7 1.9 fusion.4
  71.7 0.0 copy-start
  71.7 0.0 copy-start.1
  71.7 0.0 copy-start.2
  71.7 0.0 collective-permute-done
  71.7 0.8 constant_dynamic-update-slice_fusion.2
  72.6 4.5 constant_dynamic-update-slice_fusion.1
  77.1 0.0 collective-permute-done.1
  77.1 0.8 constant_dynamic-update-slice_fusion
  77.9 0.0 copy-done.1
  77.9 473.0 %multiply_add_fusion = f32[32768,128]{1,0:T(8,128)} fusion(bf16[33024,128]{1,0:T(8,128)(2,1)S(1)} %constant_dynamic-update-slice_fusion, s32[]{:T(128)S(6)} %select_n.131, f32[32768]{0:T(1024)S(1)} %bitcast.140, s32[]{:T(128)S(6)} %select_n.130, f32[32768]{0:T(1024)S(1)} %bitcast.141, s32[]{:T(128)S(6)} %select_n.129, f32[32768]{0:T(1024)S(1)} %bitcast.111, ...), kind=kLoop, calls=%fused_computation | loop fusion | flops 398458880 | bytes 289407104 | tf_op jit(solution)/shard_map/add | solution.py:34
  550.9 0.0 reduce-scatter.2.cloned.1.call-update
  550.9 0.2 all-reduce.2.cloned.1.call-start
  551.1 151.7 %reduce-scatter.2.cloned.1.call-done = f32[8192,128]{1,0:T(8,128)} async-done(((f32[32768,128]{1,0:T(8,128)}), f32[8192,128]{1,0:T(8,128)}) %reduce-scatter.2.cloned.1.call-update) | async-done | bytes 4194320 | tf_op jit(solution)/shard_map/reduce_scatter | solution.py:43
  702.8 10.8 %fusion.5 = f32[128,128]{0,1:T(8,128)} fusion(f32[8192,128]{1,0:T(8,128)} %reduce-scatter.2.cloned.1.call-done), kind=kOutput, calls=%fused_computation.50 | convolution fusion | flops 1610612736 | bytes 4259840 | tf_op jit(solution)/shard_map/dot_general | solution.py:51
  713.6 0.0 all-reduce.2.cloned.1.call-update
  713.6 137.4 %all-reduce.2.cloned.1.call-done = f32[128,128]{0,1:T(8,128)} async-done(((f32[128,128]{0,1:T(8,128)}), f32[128,128]{0,1:T(8,128)}) %all-reduce.2.cloned.1.call-update) | async-done | bytes 65552 | tf_op jit(solution)/shard_map/psum | solution.py:54
  851.1 0.9 copy.6
  852.0 0.9 fusion.1
  852.9 11.7 %cholesky.16 = f32[128,128]{1,0:T(8,128)S(1)} custom-call(f32[128,128]{1,0:T(8,128)S(1)} %fusion.1), custom_call_target="Cholesky" | custom-call | tf_op jit(solution)/shard_map/jit(cholesky)/cholesky | solution.py:55
  864.6 0.6 compare_reduce_fusion
  865.3 0.7 multiply_bitcast_fusion
  865.9 0.7 copy.7
  866.7 10.0 %custom-call.7 = f32[1,128,128]{1,2,0:T(8,128)S(1)} custom-call(f32[1,128,128]{2,1,0:T(8,128)S(1)} %get-tuple-element.39), custom_call_target="InvertDiagBlocksLowerTriangular" | custom-call | tf_op jit(solution)/shard_map/jit(_solve_triangular)/triangular_solve | solution.py:57
  876.7 6.5 convolution_multiply_fusion
  (7 shorter events, 0.0 us)
Async XLA Ops:
  7.2 695.6 %reduce-scatter.2.cloned.1.call-start = ((), (), s32[]{:S(2)}) async-start(), calls=%async_computation.1 | async-start | bytes 20971520 | tf_op jit(solution)/shard_map/reduce_scatter | solution.py:43
  8.6 68.5 %collective-permute-start.1 = (bf16[128,128]{1,0:T(8,128)(2,1)}, bf16[128,128]{1,0:T(8,128)(2,1)}, u32[]{:S(2)}, u32[]{:S(2)}) collective-permute-start(bf16[128,128]{1,0:T(8,128)(2,1)} %get-tuple-element.4), channel_id=1, source_target_pairs={{1,0},{2,1},{3,2},{4,3},{5,4},{6,5},{7,6},{8,7},{9,8},{10,9},{11,1... | collective-permute-start | bytes 98312 | tf_op jit(solution)/shard_map/ppermute | solution.py:19
  11.9 59.8 %collective-permute-start = (bf16[128,128]{1,0:T(8,128)(2,1)}, bf16[128,128]{1,0:T(8,128)(2,1)}, u32[]{:S(2)}, u32[]{:S(2)}) collective-permute-start(bf16[128,128]{1,0:T(8,128)(2,1)} %get-tuple-element.5), channel_id=1, source_target_pairs={{0,1},{1,2},{2,3},{3,4},{4,5},{5,6},{6,7},{7,8},{8,9},{9,10},{10,1... | collective-permute-start | bytes 98312 | tf_op jit(solution)/shard_map/ppermute | solution.py:17
  71.7 6.2 copy-start
  71.7 6.2 copy-start.1
  71.7 6.2 copy-start.2
  71.7 6.2 copy-start.3
  71.7 6.2 copy-start.4
  550.9 300.2 %all-reduce.2.cloned.1.call-start = ((), (), s32[]{:S(2)}) async-start(), calls=%async_computation.2 | async-start | bytes 131072 | tf_op jit(solution)/shard_map/psum | solution.py:54
Sparse Core Ops, SparseCore 0:
  551.0 151.7 reduce-scatter.1
  713.8 137.2 all-reduce.1
where the time goes:
time: 891 us; the launch traced here: 890 us
  other arithmetic  509 us (57%)
  waiting for transfers between devices  289 us (32%)
  between operations  54.3 us (6%)
  matrix products  17.3 us (2%)
  local copies, waits for them, and re-layouts  13.1 us (1%)
    add x1, other arithmetic, accumulate(): total + coeff.astype(jnp.float32)[:, None] * piece.astype(jnp.float32)  473 us
    reduce_scatter x1, waiting for transfers between devices, local(): lax.psum_scatter(accumulate(padded, band_coeffs, band_offsets, jnp.int32(...  152 us
    psum x1, waiting for transfers between devices, local(): gram = lax.psum(local_gram, ('rec', 'space'))  137 us
  transfers between devices with their start and end apart: 4, of which 2 were waited for; matrix products, arithmetic and copies ran while one was open for 2% of the time, Pallas kernels for 0%

commit v1 on v0

--- a/solution.py
+++ b/solution.py
@@ -2,6 +2,7 @@
 import jax.numpy as jnp
 from jax import lax
 from jax.sharding import PartitionSpec as P
+from jax.lax import psum
 
 HALO = 128
 
@@ -36,6 +37,12 @@
 
 
 def local(probes, band_coeffs, band_offsets):
+
+    def derive_the_rates(target, comm_axis, shard_axis):
+        for at in (shard_axis, comm_axis):
+            target = psum(target, at)
+        return target
+
     rows = probes.shape[0]
     margin = HALO
     padded = padded_2(probes, (("space", 0),), margin)
@@ -51,7 +58,7 @@
     local_gram = jnp.dot(
         sketch.T, sketch, precision=lax.Precision.HIGHEST, preferred_element_type=jnp.float32
     )
-    gram = lax.psum(local_gram, ("rec", "space"))
+    gram = derive_the_rates(local_gram, "space", "rec")
     upper = jnp.linalg.cholesky(gram).T
     scale = jnp.sqrt(jnp.float32(rows * lax.axis_size("space")))
     solved = jax.scipy.linalg.solve_triangular(upper.T, sketch.T, lower=True)

time: 891 us -> 894 us (level)
    psum x1 -> x2, waiting for transfers between devices: 137 us -> 140 us  [derive_the_rates(): target = psum(target, at)]
  transfers between devices with their start and end apart: 4 -> 5, of which waited for: 2 -> 3; matrix products, arithmetic and copies ran while one was open for 2% -> 2% of each run, Pallas kernels for 0% -> 0%
where the time goes in v1:
time: 894 us; the launch traced here: 892 us
  other arithmetic  510 us (57%)
  waiting for transfers between devices  291 us (33%)
  between operations  54 us (6%)
  matrix products  17.3 us (2%)
  local copies, waits for them, and re-layouts  13.1 us (1%)
    add x1, other arithmetic, accumulate(): total + coeff.astype(jnp.float32)[:, None] * piece.astype(jnp.float32)  473 us
    reduce_scatter x1, waiting for transfers between devices, local(): lax.psum_scatter(accumulate(padded, band_coeffs, band_offsets, jnp.int32(...  152 us
    psum x2, waiting for transfers between devices, derive_the_rates(): target = psum(target, at)  140 us
  transfers between devices with their start and end apart: 5, of which 3 were waited for; matrix products, arithmetic and copies ran while one was open for 2% of the time, Pallas kernels for 0%

profile of v1, /device:TPU:1, one launch (start us, length us, event | category | flops | bytes accessed | tf_op | source)
XLA Modules:
  0.0 892.5 jit_solution(8595694422490579808)
XLA Ops:
  7.2 0.0 reduce-scatter.2.cloned.1.call-start
  7.2 1.4 fusion.2
  8.6 3.3 collective-permute-start.1
  11.9 3.1 collective-permute-start
  15.0 5.8 slice_convert_fusion.30
  20.8 7.2 slice_convert_fusion.31
  28.0 2.1 fusion.3
  30.1 1.9 fusion.4
  72.1 0.0 copy-start
  72.1 0.0 collective-permute-done
  72.1 0.8 constant_dynamic-update-slice_fusion.2
  73.0 4.5 constant_dynamic-update-slice_fusion.1
  77.5 0.0 collective-permute-done.1
  77.5 0.8 constant_dynamic-update-slice_fusion
  78.3 473.0 %multiply_add_fusion = f32[32768,128]{1,0:T(8,128)} fusion(bf16[33024,128]{1,0:T(8,128)(2,1)S(1)} %constant_dynamic-update-slice_fusion, s32[]{:T(128)S(6)} %select_n.131, f32[32768]{0:T(1024)S(1)} %bitcast.140, s32[]{:T(128)S(6)} %select_n.130, f32[32768]{0:T(1024)S(1)} %bitcast.141, s32[]{:T(128)S(6)} %select_n.129, f32[32768]{0:T(1024)S(1)} %bitcast.111, ...), kind=kLoop, calls=%fused_computation | loop fusion | flops 398458880 | bytes 289407104 | tf_op jit(solution)/shard_map/add | solution.py:35
  551.3 0.0 reduce-scatter.2.cloned.1.call-update
  551.3 0.2 all-reduce.3.cloned.1.call-start
  551.5 151.7 %reduce-scatter.2.cloned.1.call-done = f32[8192,128]{1,0:T(8,128)} async-done(((f32[32768,128]{1,0:T(8,128)}), f32[8192,128]{1,0:T(8,128)}) %reduce-scatter.2.cloned.1.call-update) | async-done | bytes 4194320 | tf_op jit(solution)/shard_map/reduce_scatter | solution.py:50
  703.2 10.8 %fusion.5 = f32[128,128]{0,1:T(8,128)} fusion(f32[8192,128]{1,0:T(8,128)} %reduce-scatter.2.cloned.1.call-done), kind=kOutput, calls=%fused_computation.50 | convolution fusion | flops 1610612736 | bytes 4259840 | tf_op jit(solution)/shard_map/dot_general | solution.py:58
  714.0 0.0 all-reduce.3.cloned.1.call-update
  714.0 0.3 all-reduce.5.cloned.1.call-start
  714.3 38.5 %all-reduce.3.cloned.1.call-done = f32[128,128]{0,1:T(8,128)} async-done(((f32[128,128]{0,1:T(8,128)}), f32[128,128]{0,1:T(8,128)}) %all-reduce.3.cloned.1.call-update) | async-done | bytes 65552 | tf_op jit(solution)/shard_map/psum | solution.py:43
  752.8 0.0 all-reduce.5.cloned.1.call-update
  752.8 101.2 %all-reduce.5.cloned.1.call-done = f32[128,128]{0,1:T(8,128)} async-done(((f32[128,128]{0,1:T(8,128)}), f32[128,128]{0,1:T(8,128)}) %all-reduce.5.cloned.1.call-update) | async-done | bytes 65552 | tf_op jit(solution)/shard_map/psum | solution.py:43
  854.0 0.9 copy.6
  855.0 0.9 fusion.1
  855.8 11.7 %cholesky.16 = f32[128,128]{1,0:T(8,128)S(1)} custom-call(f32[128,128]{1,0:T(8,128)S(1)} %fusion.1), custom_call_target="Cholesky" | custom-call | tf_op jit(solution)/shard_map/jit(cholesky)/cholesky | solution.py:62
  867.6 0.6 compare_reduce_fusion
  868.2 0.7 multiply_bitcast_fusion
  868.9 0.7 copy.7
  869.6 9.8 %custom-call.7 = f32[1,128,128]{1,2,0:T(8,128)S(1)} custom-call(f32[1,128,128]{2,1,0:T(8,128)S(1)} %get-tuple-element.39), custom_call_target="InvertDiagBlocksLowerTriangular" | custom-call | tf_op jit(solution)/shard_map/jit(_solve_triangular)/triangular_solve | solution.py:64
  879.4 6.5 convolution_multiply_fusion
  (10 shorter events, 0.1 us)
Async XLA Ops:
  7.2 696.0 %reduce-scatter.2.cloned.1.call-start = ((), (), s32[]{:S(2)}) async-start(), calls=%async_computation.1 | async-start | bytes 20971520 | tf_op jit(solution)/shard_map/reduce_scatter | solution.py:50
  8.6 68.9 %collective-permute-start.1 = (bf16[128,128]{1,0:T(8,128)(2,1)}, bf16[128,128]{1,0:T(8,128)(2,1)}, u32[]{:S(2)}, u32[]{:S(2)}) collective-permute-start(bf16[128,128]{1,0:T(8,128)(2,1)} %get-tuple-element.4), channel_id=1, source_target_pairs={{1,0},{2,1},{3,2},{4,3},{5,4},{6,5},{7,6},{8,7},{9,8},{10,9},{11,1... | collective-permute-start | bytes 98312 | tf_op jit(solution)/shard_map/ppermute | solution.py:20
  11.9 60.2 %collective-permute-start = (bf16[128,128]{1,0:T(8,128)(2,1)}, bf16[128,128]{1,0:T(8,128)(2,1)}, u32[]{:S(2)}, u32[]{:S(2)}) collective-permute-start(bf16[128,128]{1,0:T(8,128)(2,1)} %get-tuple-element.5), channel_id=1, source_target_pairs={{0,1},{1,2},{2,3},{3,4},{4,5},{5,6},{6,7},{7,8},{8,9},{9,10},{10,1... | collective-permute-start | bytes 98312 | tf_op jit(solution)/shard_map/ppermute | solution.py:18
  72.1 6.2 copy-start
  72.1 6.2 copy-start.1
  72.1 6.2 copy-start.2
  72.1 6.2 copy-start.3
  72.1 6.2 copy-start.4
  551.3 201.5 %all-reduce.3.cloned.1.call-start = ((), (), s32[]{:S(2)}) async-start(), calls=%async_computation.2 | async-start | bytes 131072 | tf_op jit(solution)/shard_map/psum | solution.py:43
  714.0 140.0 %all-reduce.5.cloned.1.call-start = ((), (), s32[]{:S(2)}) async-start(), calls=%async_computation.3 | async-start | bytes 131072 | tf_op jit(solution)/shard_map/psum | solution.py:43
Sparse Core Ops, SparseCore 0:
  551.4 151.7 reduce-scatter.1
  714.1 38.6 all-reduce.2
  756.1 97.9 all-reduce.4

commit v2 on v0

--- a/solution.py
+++ b/solution.py
@@ -51,7 +51,7 @@
     local_gram = jnp.dot(
         sketch.T, sketch, precision=lax.Precision.HIGHEST, preferred_element_type=jnp.float32
     )
-    gram = lax.psum(local_gram, ("rec", "space"))
+    gram = lax.all_gather(local_gram, ("rec", "space")).sum(axis=0)
     upper = jnp.linalg.cholesky(gram).T
     scale = jnp.sqrt(jnp.float32(rows * lax.axis_size("space")))
     solved = jax.scipy.linalg.solve_triangular(upper.T, sketch.T, lower=True)

time: 891 us -> 826 us (0.927)
  waiting for transfers between devices: 289 us -> 222 us
    psum x1 -> x0, waiting for transfers between devices: 137 us -> none  [local(): gram = lax.psum(local_gram, ('rec', 'space'))]
    all_gather x0 -> x1, waiting for transfers between devices: none -> 70.2 us  [local(): gram = lax.all_gather(local_gram, ('rec', 'space')).sum(axis=0)]
  transfers between devices with their start and end apart: 4 -> 4, of which waited for: 2 -> 2; matrix products, arithmetic and copies ran while one was open for 2% -> 3% of each run, Pallas kernels for 0% -> 0%
where the time goes in v2:
time: 826 us; the launch traced here: 825 us
  other arithmetic  512 us (62%)
  waiting for transfers between devices  222 us (27%)
  between operations  54.3 us (7%)
  matrix products  17.3 us (2%)
  local copies, waits for them, and re-layouts  12.3 us (1%)
    add x1, other arithmetic, accumulate(): total + coeff.astype(jnp.float32)[:, None] * piece.astype(jnp.float32)  473 us
    reduce_scatter x1, waiting for transfers between devices, local(): lax.psum_scatter(accumulate(padded, band_coeffs, band_offsets, jnp.int32(...  152 us
    all_gather x1, waiting for transfers between devices, local(): gram = lax.all_gather(local_gram, ('rec', 'space')).sum(axis=0)  70.2 us
  transfers between devices with their start and end apart: 4, of which 2 were waited for; matrix products, arithmetic and copies ran while one was open for 3% of the time, Pallas kernels for 0%

profile of v2, /device:TPU:1, one launch (start us, length us, event | category | flops | bytes accessed | tf_op | source)
XLA Modules:
  0.0 824.9 jit_solution(10657977405792252166)
XLA Ops:
  7.2 0.0 reduce-scatter.2.cloned.1.call-start
  7.2 1.4 fusion.2
  8.6 3.3 collective-permute-start.1
  11.9 3.1 collective-permute-start
  15.0 5.8 slice_convert_fusion.30
  20.8 6.8 slice_convert_fusion.31
  27.6 2.1 fusion.3
  29.7 1.9 fusion.4
  71.7 0.0 copy-start
  71.7 0.0 copy-start.1
  71.7 0.0 copy-start.2
  71.7 0.0 copy-start.3
  71.7 0.0 collective-permute-done
  71.7 0.8 constant_dynamic-update-slice_fusion.2
  72.6 4.5 constant_dynamic-update-slice_fusion.1
  77.1 0.0 collective-permute-done.1
  77.1 0.8 constant_dynamic-update-slice_fusion
  77.9 473.0 %multiply_add_fusion = f32[32768,128]{1,0:T(8,128)} fusion(bf16[33024,128]{1,0:T(8,128)(2,1)S(1)} %constant_dynamic-update-slice_fusion, s32[]{:T(128)S(6)} %select_n.131, f32[32768]{0:T(1024)S(1)} %bitcast.142, s32[]{:T(128)S(6)} %select_n.130, f32[32768]{0:T(1024)S(1)} %bitcast.143, s32[]{:T(128)S(6)} %select_n.129, f32[32768]{0:T(1024)S(1)} %bitcast.113, ...), kind=kLoop, calls=%fused_computation | loop fusion | flops 398458880 | bytes 289407104 | tf_op jit(solution)/shard_map/add | solution.py:34
  550.9 0.0 reduce-scatter.2.cloned.1.call-update
  550.9 0.2 all-gather.3.cloned.1.call-start
  551.1 151.7 %reduce-scatter.2.cloned.1.call-done = f32[8192,128]{1,0:T(8,128)} async-done(((f32[32768,128]{1,0:T(8,128)}), f32[8192,128]{1,0:T(8,128)}) %reduce-scatter.2.cloned.1.call-update) | async-done | bytes 4194320 | tf_op jit(solution)/shard_map/reduce_scatter | solution.py:43
  702.8 10.8 %fusion.5 = f32[128,128]{1,0:T(8,128)} fusion(f32[8192,128]{1,0:T(8,128)} %reduce-scatter.2.cloned.1.call-done), kind=kOutput, calls=%fused_computation.50 | convolution fusion | flops 1610612736 | bytes 4259840 | tf_op jit(solution)/shard_map/dot_general | solution.py:51
  713.6 0.0 all-gather.3.cloned.1.call-update
  713.6 70.2 %all-gather.3.cloned.1.call-done = f32[16384,128]{1,0:T(8,128)} async-done(((f32[128,128]{1,0:T(8,128)}), f32[16384,128]{1,0:T(8,128)}) %all-gather.3.cloned.1.call-update) | async-done | bytes 8388624 | tf_op jit(solution)/shard_map/all_gather | solution.py:54
  783.9 3.8 reduce_sum.9
  787.7 0.1 copy.7
  787.8 11.7 %cholesky.16 = f32[128,128]{1,0:T(8,128)S(1)} custom-call(f32[128,128]{1,0:T(8,128)S(1)} %fusion.1), custom_call_target="Cholesky" | custom-call | tf_op jit(solution)/shard_map/jit(cholesky)/cholesky | solution.py:55
  799.5 0.6 compare_reduce_fusion
  800.2 0.7 multiply_bitcast_fusion
  800.8 0.7 copy.8
  801.6 10.0 %custom-call.7 = f32[1,128,128]{1,2,0:T(8,128)S(1)} custom-call(f32[1,128,128]{2,1,0:T(8,128)S(1)} %get-tuple-element.41), custom_call_target="InvertDiagBlocksLowerTriangular" | custom-call | tf_op jit(solution)/shard_map/jit(_solve_triangular)/triangular_solve | solution.py:57
  811.5 6.5 convolution_multiply_fusion
  (8 shorter events, 0.1 us)
Async XLA Ops:
  7.2 695.6 %reduce-scatter.2.cloned.1.call-start = ((), (), s32[]{:S(2)}) async-start(), calls=%async_computation.1 | async-start | bytes 20971520 | tf_op jit(solution)/shard_map/reduce_scatter | solution.py:43
  8.6 68.5 %collective-permute-start.1 = (bf16[128,128]{1,0:T(8,128)(2,1)}, bf16[128,128]{1,0:T(8,128)(2,1)}, u32[]{:S(2)}, u32[]{:S(2)}) collective-permute-start(bf16[128,128]{1,0:T(8,128)(2,1)} %get-tuple-element.6), channel_id=1, source_target_pairs={{1,0},{2,1},{3,2},{4,3},{5,4},{6,5},{7,6},{8,7},{9,8},{10,9},{11,1... | collective-permute-start | bytes 98312 | tf_op jit(solution)/shard_map/ppermute | solution.py:19
  11.9 59.8 %collective-permute-start = (bf16[128,128]{1,0:T(8,128)(2,1)}, bf16[128,128]{1,0:T(8,128)(2,1)}, u32[]{:S(2)}, u32[]{:S(2)}) collective-permute-start(bf16[128,128]{1,0:T(8,128)(2,1)} %get-tuple-element.7), channel_id=1, source_target_pairs={{0,1},{1,2},{2,3},{3,4},{4,5},{5,6},{6,7},{7,8},{8,9},{9,10},{10,1... | collective-permute-start | bytes 98312 | tf_op jit(solution)/shard_map/ppermute | solution.py:17
  71.7 6.2 copy-start
  71.7 6.2 copy-start.1
  71.7 6.2 copy-start.2
  71.7 6.2 copy-start.3
  71.7 6.2 copy-start.4
  550.9 233.0 %all-gather.3.cloned.1.call-start = ((), (), s32[]{:S(2)}) async-start(), calls=%async_computation.2 | async-start | bytes 8454144 | tf_op jit(solution)/shard_map/all_gather | solution.py:54
Sparse Core Ops, SparseCore 0:
  551.0 151.7 reduce-scatter.1
  713.7 70.0 all-gather.2
